TPU v7x, 256 devices: a whole 4x4x8 slice. The times are simulated.
256 devices in a mesh: dp: 2 (over core), seq: 32 (over z, x), mp: 4 (over y).
Axes of the slice: x: 4, y: 4, z: 8, core: 2. Of those that a mesh axis runs over, the one named last changes fastest.
Arguments:
- queries: bfloat16 [6, 4096, 4096], P('dp', 'seq', 'mp'), may hold values from -1000 to 1000
- database: bfloat16 [1024, 128, 1024], P('seq', None, 'mp'), may hold values from -300 to 300
- owner_ids: int32 [2, 32, 6, 2], P('dp'), may hold values from 0 to 31, all different within a row; in each aligned block of 6 rows (0 to 5, 6 to 11, ..., all dimensions but the last counted through in order) at most 2 rows name the same one
- row_ids: int32 [2, 32, 6, 2], P('dp'), may hold values from 0 to 31
- pre_gain: float32 [1024], replicated, may hold values from 0.1 to 1.9
- out_gain: float32 [1024], replicated, may hold values from 0.1 to 1.9
- w_in: bfloat16 [1024, 4096], P(None, 'mp'), may hold values from -0.1875 to 0.1875
- w_out: bfloat16 [4096, 1024], P('mp'), may hold values from -0.09375 to 0.09375
- w_key: bfloat16 [1024, 4096], P(None, 'mp'), may hold values from -0.1875 to 0.1875
- w_value: bfloat16 [1024, 4096], P(None, 'mp'), may hold values from -0.1875 to 0.1875
Outputs:
- attended: bfloat16 [6, 4096, 4096], P('dp', 'seq', 'mp')
Inputs may be any that keep to these rules, and one draw needn't show every extreme that they name: `owner_ids`: within one index pair of the first two dimensions (the 6 spans of one device) no shard number appears more than 2 times, and the 2 neighbours of one span lie on different shards.
All inputs are finite; a program needn't handle non-finite values.
Results may differ from a plain program's by a relative error of at most 0.04.
Values may be sent and summed in bfloat16 or wider, within the bound.
No kernel may reach another device: no remote copies, remote signals or barrier semaphores. Data moves between devices by JAX's collectives and lax.ppermute only.
A program may use at most 64 MiB of HBM per device.

v0:
```python
import jax
import jax.numpy as jnp
from jax import lax
from jax.sharding import PartitionSpec as P

HD = 128
MOST = 2
epsilon = 1e-06


def passed_along(array, axis, by):
    peers = lax.axis_size(axis)
    pairs = [(i, i + by) for i in range(peers) if 0 <= i + by < peers]
    return lax.ppermute(array, axis, pairs)


def rms_scale(values, gain_values):
    return (
        values
        * lax.rsqrt(jnp.mean(values * values, axis=-1, keepdims=True) + epsilon)
        * gain_values
    )


def body(queries, database, owner_ids, row_ids, pre_gain, out_gain, w_in, w_out, w_key, w_value):
    shards = lax.axis_size("seq")
    my_index = lax.axis_index("seq")
    seq_count, length, local_width = queries.shape
    slot_count = owner_ids.shape[2]
    per_span = slot_count // seq_count
    neigh_count = owner_ids.shape[3]
    block_len = database.shape[1]
    requests = slot_count * neigh_count
    owners = owner_ids[0].reshape(shards, requests)
    row_index = row_ids[0].reshape(shards, requests)
    position = jnp.arange(requests)
    before = position[None, :] < position[:, None]
    slot_rank = jnp.sum((owners[:, :, None] == owners[:, None, :]) & before[None], axis=2)
    own_owner = lax.dynamic_index_in_dim(owners, my_index, 0, keepdims=False)
    own_rank = lax.dynamic_index_in_dim(slot_rank, my_index, 0, keepdims=False)
    is_mine = (owners == my_index)[:, None, :] & (
        slot_rank[:, None, :] == jnp.arange(MOST)[:, None]
    )
    wanted = jnp.sum(jnp.where(is_mine, row_index[:, None, :], 0), axis=2)
    sending = jnp.take(database, wanted.reshape(-1), axis=0)
    arrived = lax.all_to_all(
        sending.reshape((shards, MOST) + database.shape[1:]),
        "seq",
        split_axis=0,
        concat_axis=0,
        tiled=True,
    )
    stacked = arrived.reshape((shards * MOST,) + arrived.shape[2:])
    blocks = jnp.take(stacked, own_owner * MOST + own_rank, axis=0)
    blocks = blocks.reshape((seq_count, per_span, neigh_count, block_len, blocks.shape[-1]))
    arrived_rows = passed_along(blocks[:, -1], "seq", 1)
    blocks = jnp.concatenate([arrived_rows[:, None], blocks[:, :-1]], axis=1)
    blocks = lax.all_gather(blocks, "mp", axis=4, tiled=True)
    features = blocks.shape[-1]
    widened = blocks.reshape(-1, features).astype(jnp.float32)
    normed = rms_scale(widened, pre_gain).astype(jnp.bfloat16)
    hidden_act = jax.nn.gelu(jnp.dot(normed, w_in, preferred_element_type=jnp.float32)).astype(
        jnp.bfloat16
    )
    summed = lax.psum(
        jnp.dot(hidden_act, w_out, preferred_element_type=jnp.float32).astype(jnp.bfloat16), "mp"
    ).astype(jnp.float32)
    encoded = rms_scale(widened + summed, out_gain).astype(jnp.bfloat16)
    key_rows = jnp.dot(encoded, w_key, preferred_element_type=jnp.float32).astype(jnp.bfloat16)
    value_rows = jnp.dot(encoded, w_value, preferred_element_type=jnp.float32).astype(jnp.bfloat16)
    key_rows = key_rows.reshape(seq_count, per_span, neigh_count * block_len, local_width)
    value_rows = value_rows.reshape(seq_count, per_span, neigh_count * block_len, local_width)
    head_count = local_width // HD
    span_len = length // per_span
    query_rows = queries.reshape(seq_count, per_span, span_len, head_count, HD)
    key_rows = key_rows.reshape(seq_count, per_span, neigh_count * block_len, head_count, HD)
    value_rows = value_rows.reshape(seq_count, per_span, neigh_count * block_len, head_count, HD)
    scores = jnp.einsum(
        "scqhd,sckhd->schqk", query_rows, key_rows, preferred_element_type=jnp.float32
    ) * HD ** (-0.5)
    scores = scores - jnp.max(scores, axis=-1, keepdims=True)
    weights = jnp.exp(scores)
    weights = (weights / jnp.sum(weights, axis=-1, keepdims=True)).astype(jnp.bfloat16)
    attended = jnp.einsum(
        "schqk,sckhd->scqhd", weights, value_rows, preferred_element_type=jnp.float32
    )
    has_source = my_index * per_span + jnp.arange(per_span) > 0
    attended = jnp.where(has_source[None, :, None, None, None], attended, 0.0)
    return attended.astype(jnp.bfloat16).reshape(seq_count, length, local_width)


def solution(mesh):
    return jax.shard_map(
        body,
        mesh=mesh,
        in_specs=(
            P("dp", "seq", "mp"),
            P("seq", None, "mp"),
            P("dp", None, None, None),
            P("dp", None, None, None),
            P(),
            P(),
            P(None, "mp"),
            P("mp", None),
            P(None, "mp"),
            P(None, "mp"),
        ),
        out_specs=P("dp", "seq", "mp"),
        check_vma=False,
    )
```

profile of v0, /device:TPU:1, one launch (start us, length us, event | category | flops | bytes accessed | tf_op | source)
XLA Modules:
  0.0 324.7 jit_solution(9118255975437345221)
XLA Ops:
  6.5 0.8 reshape_squeeze.3
  7.5 0.7 broadcast_in_dim.63
  8.6 2.8 gather_fusion
  11.4 4.5 %broadcast_select_fusion = bf16[32,2,128,256]{3,2,1,0:T(8,128)(2,1)} fusion(bf16[32,2,128,256]{3,2,1,0:T(8,128)(2,1)} %bitcast.73, pred[32,2]{1,0:T(8,128)(4,1)S(1)} %copy.37), kind=kLoop, calls=%fused_computation.20 | loop fusion | flops 2097152 | bytes 8388672 | tf_op jit(solution)/shard_map/jit(_take)/select_n | solution.py:45
  15.9 12.0 %all-to-all-start = ((bf16[32,2,128,256]{3,2,1,0:T(8,128)(2,1)}), bf16[32,2,128,256]{3,2,1,0:T(8,128)(2,1)}, u32[]{:S(2)}, u32[]{:S(2)}) async-start(bf16[32,2,128,256]{3,2,1,0:T(8,128)(2,1)} %broadcast_select_fusion), calls=%async_computation | async-start | bytes 8388608 | tf_op jit(solution)/shard_map/all_to_all | solution.py:46
  28.0 0.2 add_reduce_fusion
  28.3 92.7 %all-to-all-done = bf16[32,2,128,256]{3,2,1,0:T(8,128)(2,1)} async-done(((bf16[32,2,128,256]{3,2,1,0:T(8,128)(2,1)}), bf16[32,2,128,256]{3,2,1,0:T(8,128)(2,1)}, u32[]{:S(2)}, u32[]{:S(2)}) %all-to-all-start) | async-done | bytes 4194336 | tf_op jit(solution)/shard_map/all_to_all | solution.py:46
  121.0 2.8 gather_fusion.1
  123.7 0.1 broadcast_select_fusion.1
  124.0 4.6 %collective-permute-start = (bf16[3,2,128,256]{3,2,1,0:T(8,128)(2,1)S(1)}, bf16[3,2,128,256]{3,2,1,0:T(8,128)(2,1)S(1)}, u32[]{:S(2)}, u32[]{:S(2)}) collective-permute-start(bf16[3,2,128,256]{3,2,1,0:T(8,128)(2,1)S(1)} %get-tuple-element.5), channel_id=1, source_target_pairs={{0,4},{4,8},{8,12},{12,16},{16,20},{20,24},{24,28},{28,32},{32,36}... | collective-permute-start | bytes 1179656 | tf_op jit(solution)/shard_map/ppermute | solution.py:14
  128.6 5.2 %collective-permute-done = bf16[3,2,128,256]{3,2,1,0:T(8,128)(2,1)S(1)} collective-permute-done((bf16[3,2,128,256]{3,2,1,0:T(8,128)(2,1)S(1)}, bf16[3,2,128,256]{3,2,1,0:T(8,128)(2,1)S(1)}, u32[]{:S(2)}, u32[]{:S(2)}) %collective-permute-start) | collective-permute-done | bytes 393248 | tf_op jit(solution)/shard_map/ppermute | solution.py:14
  133.7 0.9 pad_maximum_fusion
  134.8 47.7 %all-gather.2.cloned.1.call-done = bf16[3,2,2,128,1024]{4,3,2,1,0:T(8,128)(2,1)} async-done(((bf16[3,2,2,128,256]{4,3,2,1,0:T(8,128)(2,1)}), bf16[3,2,2,128,1024]{4,3,2,1,0:T(8,128)(2,1)}) %all-gather.2.cloned.1.call-update) | async-done | bytes 3145744 | tf_op jit(solution)/shard_map/all_gather | solution.py:58
  182.5 2.6 fusion.9
  185.1 4.4 %fusion.11 = bf16[1536,1024]{1,0:T(8,128)(2,1)} fusion(bf16[3,2,2,128,1024]{4,3,2,1,0:T(8,128)(2,1)} %all-gather.2.cloned.1.call-done, f32[1024]{0:T(1024)S(1)} %copy-done.5, f32[1536]{0:T(1024)S(1)} %rsqrt.20), kind=kLoop, calls=%fused_computation.17 | loop fusion | flops 6291456 | bytes 6301696 | tf_op jit(solution)/shard_map/convert_element_type | solution.py:61
  189.5 10.9 %convolution_convert_fusion.2 = bf16[1536,1024]{1,0:T(8,128)(2,1)} fusion(bf16[1024,1024]{1,0:T(8,128)(2,1)} %param.17, bf16[1536,1024]{1,0:T(8,128)(2,1)} %fusion.11, bf16[1024,1024]{1,0:T(8,128)(2,1)} %param.16), kind=kOutput, calls=%fused_computation.23 | convolution fusion | flops 6458179584 | bytes 10485760 | tf_op jit(solution)/shard_map/dot_general | solution.py:66
  200.4 1.3 copy.46
  201.8 81.8 %all-reduce.2.cloned.1.call-done = bf16[1536,1024]{1,0:T(8,128)(2,1)} async-done(((bf16[1536,1024]{1,0:T(8,128)(2,1)}), bf16[1536,1024]{1,0:T(8,128)(2,1)}) %all-reduce.2.cloned.1.call-update) | async-done | bytes 3145744 | tf_op jit(solution)/shard_map/psum | solution.py:65
  283.6 4.1 %multiply_reduce_fusion = f32[1536]{0:T(1024)S(1)} fusion(bf16[1536,1024]{1,0:T(8,128)(2,1)} %all-reduce.2.cloned.1.call-done, bf16[3,2,2,128,1024]{4,3,2,1,0:T(8,128)(2,1)} %all-gather.2.cloned.1.call-done), kind=kLoop, calls=%fused_computation.19 | loop fusion | flops 7862784 | bytes 6297600 | tf_op jit(solution)/shard_map/reduce_sum | solution.py:20
  287.7 0.6 copy-done.2
  288.3 1.1 multiply_convert_fusion
  289.4 0.4 copy-done.6
  289.9 3.6 %fusion.27 = bf16[192,8,8,128]{3,1,2,0:T(8,128)(2,1)S(1)} fusion(bf16[1536,1024]{1,0:T(8,128)(2,1)S(1)} %multiply_convert_fusion, bf16[1024,1024]{1,0:T(8,128)(2,1)S(1)} %copy-done.6), kind=kOutput, calls=%fused_computation.39 | convolution fusion | flops 3222798336 | bytes 8388608 | tf_op jit(solution)/shard_map/dot_general | solution.py:69
  293.5 0.8 copy.45
  294.3 1.2 fusion.17
  295.6 1.1 fusion.51
  296.7 1.6 copy-done.7
  298.3 3.9 %fusion.26 = bf16[192,8,8,128]{3,1,2,0:T(8,128)(2,1)S(1)} fusion(bf16[1536,1024]{1,0:T(8,128)(2,1)S(1)} %multiply_convert_fusion, bf16[1024,1024]{1,0:T(8,128)(2,1)S(1)} %copy-done.7), kind=kOutput, calls=%fused_computation.38 | convolution fusion | flops 3222798336 | bytes 8388608 | tf_op jit(solution)/shard_map/dot_general | solution.py:70
  302.1 2.5 copy.47
  304.6 10.3 %fusion.32 = bf16[3,2,64,8,128]{4,2,3,1,0:T(8,128)(2,1)} fusion(bf16[3,2,256,8,128]{4,3,2,1,0:T(8,128)(2,1)} %bitcast.76, f32[3,2,8,64]{3,2,1,0:T(8,128)S(1)} %fusion.51, pred[2]{0:T(512)(128)(4,1)S(1)} %add_compare_fusion, f32[3,2,8,256,64]{3,4,2,1,0:T(8,128)} %copy-done.3), kind=kOutput, calls=%fused_computation.43 | convolution fusion | flops 206048512 | bytes 7090178 | tf_op jit(solution)/shard_map/schqk,sckhd->scqhd/dot_general | solution.py:84
  315.0 1.7 copy.43
  316.6 1.2 reshape.158
  (36 shorter events, 0.8 us)
Async XLA Ops:
  6.5 2.0 copy-start
  15.9 105.0 %all-to-all-start = ((bf16[32,2,128,256]{3,2,1,0:T(8,128)(2,1)}), bf16[32,2,128,256]{3,2,1,0:T(8,128)(2,1)}, u32[]{:S(2)}, u32[]{:S(2)}) async-start(bf16[32,2,128,256]{3,2,1,0:T(8,128)(2,1)} %broadcast_select_fusion), calls=%async_computation | async-start | bytes 8388608 | tf_op jit(solution)/shard_map/all_to_all | solution.py:46
  27.9 154.6 %all-gather.2.cloned.1.call-start = ((), (), s32[]{:S(2)}) async-start(), calls=%async_computation.1 | async-start | bytes 3932160 | tf_op jit(solution)/shard_map/all_gather | solution.py:58
  124.0 61.1 %copy-start.5 = (f32[1024]{0:T(1024)S(1)}, f32[1024]{0:T(1024)}, u32[]{:S(2)}) copy-start(f32[1024]{0:T(1024)} %param.14) | copy-start | bytes 12292
  124.0 9.8 %collective-permute-start = (bf16[3,2,128,256]{3,2,1,0:T(8,128)(2,1)S(1)}, bf16[3,2,128,256]{3,2,1,0:T(8,128)(2,1)S(1)}, u32[]{:S(2)}, u32[]{:S(2)}) collective-permute-start(bf16[3,2,128,256]{3,2,1,0:T(8,128)(2,1)S(1)} %get-tuple-element.5), channel_id=1, source_target_pairs={{0,4},{4,8},{8,12},{12,16},{16,20},{20,24},{24,28},{28,32},{32,36}... | collective-permute-start | bytes 1179656 | tf_op jit(solution)/shard_map/ppermute | solution.py:14
  134.7 148.9 %all-reduce.2.cloned.1.call-start = ((), (), s32[]{:S(2)}) async-start(), calls=%async_computation.2 | async-start | bytes 6291456 | tf_op jit(solution)/shard_map/psum | solution.py:65
  201.7 85.9 %copy-start.4 = (f32[1024]{0:T(1024)S(1)}, f32[1024]{0:T(1024)}, u32[]{:S(2)}) copy-start(f32[1024]{0:T(1024)} %param.15) | copy-start | bytes 12292
  283.6 4.1 %copy-start.1 = (bf16[3,2,2,128,1024]{4,3,2,1,0:T(8,128)(2,1)S(1)}, bf16[3,2,2,128,1024]{4,3,2,1,0:T(8,128)(2,1)}, u32[]{:S(2)}) copy-start(bf16[3,2,2,128,1024]{4,3,2,1,0:T(8,128)(2,1)} %all-gather.2.cloned.1.call-done) | copy-start | bytes 9437188
  283.6 4.7 %copy-start.2 = (bf16[1536,1024]{1,0:T(8,128)(2,1)S(1)}, bf16[1536,1024]{1,0:T(8,128)(2,1)}, u32[]{:S(2)}) copy-start(bf16[1536,1024]{1,0:T(8,128)(2,1)} %all-reduce.2.cloned.1.call-done) | copy-start | bytes 9437188
  288.3 1.6 copy-start.6
  295.5 6.6 %copy-start.3 = (f32[3,2,8,256,64]{3,4,2,1,0:T(8,128)}, f32[3,2,8,256,64]{3,4,2,1,0:T(8,128)S(1)}, u32[]{:S(2)}) copy-start(f32[3,2,8,256,64]{3,4,2,1,0:T(8,128)S(1)} %fusion.17) | copy-start | bytes 9437188
  295.5 2.7 copy-start.7
Sparse Core Ops, SparseCore 0:
  134.8 47.5 all-gather.1
  200.5 82.9 all-reduce.1
where the time goes:
time: 325 us
  waiting for transfers between devices  227 us (70%)
  matrix products  29.9 us (9%)
  other arithmetic  19.3 us (6%)
  local copies, waits for them, and re-layouts  17.7 us (5%)
  starting transfers between devices  16.7 us (5%)
  between operations  13.6 us (4%)
    all_to_all x1, waiting for transfers between devices, body(): lax.all_to_all(sending.reshape((shards, MOST) + database.shape[1:]), 'seq...  92.7 us
    psum x1, waiting for transfers between devices, body(): lax.psum(jnp.dot(hidden_act, w_out, preferred_element_type=jnp.float32).a...  81.8 us
    all_gather x1, waiting for transfers between devices, body(): blocks = lax.all_gather(blocks, 'mp', axis=4, tiled=True)  47.7 us
    all_to_all x1, starting transfers between devices, body(): lax.all_to_all(sending.reshape((shards, MOST) + database.shape[1:]), 'seq...  12 us
    dot_general x1, matrix products, body(): jnp.dot(hidden_act, w_out, preferred_element_type=jnp.float32)  10.9 us
    dot_general x1, matrix products, body(): jnp.einsum('schqk,sckhd->scqhd', weights, value_rows, preferred_element_t...  10.3 us
    unnamed x19, local copies, waits for them, and re-layouts  7.25 us
    reduce_sum x2, other arithmetic, rms_scale(): jnp.mean(values * values, axis=-1, keepdims=True) + epsilon  6.65 us
  transfers between devices with their start and end apart: 4, of which 4 were waited for; matrix products, arithmetic and copies ran while one was open for 0% of the time, Pallas kernels for 0%

commit v1 on v0

--- a/solution.py
+++ b/solution.py
@@ -1,3 +1,4 @@
+import functools
 import jax
 import jax.numpy as jnp
 from jax import lax
@@ -6,6 +7,35 @@
 HD = 128
 MOST = 2
 epsilon = 1e-06
+
+
+def fix_the_stocks(packet, d_out):
+    long_array = list(packet.shape[1:])
+    long_array[d_out] *= packet.shape[0]
+    back = jnp.moveaxis(packet, 0, d_out).reshape(long_array)
+    return back
+
+
+def point_the_routes_all(state, named_axis):
+    z1 = state[None]
+    n_axis = lax.axis_size(named_axis)
+    for p in range(n_axis.bit_length() - 1):
+        q_next = 1 << p
+        outer = lax.ppermute(
+            z1, axis_name=named_axis, perm=[(no, no ^ q_next) for no in range(n_axis)]
+        )
+        g_now = jnp.stack([z1, outer])
+        then = lax.axis_index(named_axis) >> p & 1
+        z1 = jnp.where(then == 0, g_now, g_now[::-1]).reshape(-1, *state.shape)
+    return z1
+
+
+def treat_domain_on_mesh(point, sample, dim_i):
+    upper = fix_the_stocks(point_the_routes_all(point, sample), dim_i)
+    return upper
+
+
+core_supply_all = functools.partial(treat_domain_on_mesh, sample="mp", dim_i=4)
 
 
 def passed_along(array, axis, by):
@@ -55,7 +85,7 @@
     blocks = blocks.reshape((seq_count, per_span, neigh_count, block_len, blocks.shape[-1]))
     arrived_rows = passed_along(blocks[:, -1], "seq", 1)
     blocks = jnp.concatenate([arrived_rows[:, None], blocks[:, :-1]], axis=1)
-    blocks = lax.all_gather(blocks, "mp", axis=4, tiled=True)
+    blocks = core_supply_all(blocks)
     features = blocks.shape[-1]
     widened = blocks.reshape(-1, features).astype(jnp.float32)
     normed = rms_scale(widened, pre_gain).astype(jnp.bfloat16)

time: 325 us -> 348 us (1.071)
  local copies, waits for them, and re-layouts: 17.7 us -> 27.8 us
  waiting for transfers between devices: 227 us -> 232 us
  starting transfers between devices: 16.7 us -> 20.9 us
  other arithmetic: 19.3 us -> 23 us
    all_gather x1 -> x0, waiting for transfers between devices: 47.7 us -> none  [body(): blocks = lax.all_gather(blocks, 'mp', axis=4, tiled=True)]
    ppermute x0 -> x2, waiting for transfers between devices: none -> 45.1 us  [point_the_routes_all(): lax.ppermute(z1, axis_name=named_axis, perm=[(no, no ^ q_next) for no in...]
    psum x1, waiting for transfers between devices: 81.8 us -> 88.7 us  [body(): lax.psum(jnp.dot(hidden_act, w_out, preferred_element_type=jnp.float32).a...]
    convert_element_type x0 -> x1, local copies, waits for them, and re-layouts: none -> 6.85 us  [body(): widened = blocks.reshape(-1, features).astype(jnp.float32)]
    ppermute x0 -> x2, starting transfers between devices: none -> 4.3 us  [point_the_routes_all(): lax.ppermute(z1, axis_name=named_axis, perm=[(no, no ^ q_next) for no in...]
    another operation x0 -> x4, other arithmetic: none -> 3.62 us  [point_the_routes_all(): g_now = jnp.stack([z1, outer])]
    unnamed x19 -> x22, local copies, waits for them, and re-layouts: 7.25 us -> 10.5 us
  transfers between devices with their start and end apart: 4 -> 5, of which waited for: 4 -> 5; matrix products, arithmetic and copies ran while one was open for 0% -> 0% of each run, Pallas kernels for 0% -> 0%
where the time goes in v1:
time: 348 us
  waiting for transfers between devices  232 us (67%)
  matrix products  30.7 us (9%)
  local copies, waits for them, and re-layouts  27.8 us (8%)
  other arithmetic  23 us (7%)
  starting transfers between devices  20.9 us (6%)
  between operations  13.7 us (4%)
    all_to_all x1, waiting for transfers between devices, body(): lax.all_to_all(sending.reshape((shards, MOST) + database.shape[1:]), 'seq...  92.7 us
    psum x1, waiting for transfers between devices, body(): lax.psum(jnp.dot(hidden_act, w_out, preferred_element_type=jnp.float32).a...  88.7 us
    ppermute x2, waiting for transfers between devices, point_the_routes_all(): lax.ppermute(z1, axis_name=named_axis, perm=[(no, no ^ q_next) for no in...  45.1 us
    all_to_all x1, starting transfers between devices, body(): lax.all_to_all(sending.reshape((shards, MOST) + database.shape[1:]), 'seq...  12 us
    dot_general x1, matrix products, body(): jnp.dot(hidden_act, w_out, preferred_element_type=jnp.float32)  11.6 us
    unnamed x22, local copies, waits for them, and re-layouts  10.5 us
    dot_general x1, matrix products, body(): jnp.einsum('schqk,sckhd->scqhd', weights, value_rows, preferred_element_t...  10.4 us
  transfers between devices with their start and end apart: 5, of which 5 were waited for; matrix products, arithmetic and copies ran while one was open for 0% of the time, Pallas kernels for 0%

profile of v1, /device:TPU:1, one launch (start us, length us, event | category | flops | bytes accessed | tf_op | source)
XLA Modules:
  0.0 347.8 jit_solution(7676948731739661471)
XLA Ops:
  6.5 0.8 reshape_squeeze.3
  8.6 2.8 gather_fusion
  11.4 4.5 %broadcast_select_fusion = bf16[32,2,128,256]{3,2,1,0:T(8,128)(2,1)} fusion(bf16[32,2,128,256]{3,2,1,0:T(8,128)(2,1)} %bitcast.81, pred[32,2]{1,0:T(8,128)(4,1)S(1)} %copy.41), kind=kLoop, calls=%fused_computation.18 | loop fusion | flops 2097152 | bytes 8388672 | tf_op jit(solution)/shard_map/jit(_take)/select_n | solution.py:75
  15.9 12.0 %all-to-all-start = ((bf16[32,2,128,256]{3,2,1,0:T(8,128)(2,1)}), bf16[32,2,128,256]{3,2,1,0:T(8,128)(2,1)}, u32[]{:S(2)}, u32[]{:S(2)}) async-start(bf16[32,2,128,256]{3,2,1,0:T(8,128)(2,1)} %broadcast_select_fusion), calls=%async_computation | async-start | bytes 8388608 | tf_op jit(solution)/shard_map/all_to_all | solution.py:76
  28.3 92.7 %all-to-all-done = bf16[32,2,128,256]{3,2,1,0:T(8,128)(2,1)} async-done(((bf16[32,2,128,256]{3,2,1,0:T(8,128)(2,1)}), bf16[32,2,128,256]{3,2,1,0:T(8,128)(2,1)}, u32[]{:S(2)}, u32[]{:S(2)}) %all-to-all-start) | async-done | bytes 4194336 | tf_op jit(solution)/shard_map/all_to_all | solution.py:76
  121.0 2.8 gather_fusion.1
  124.0 4.6 %collective-permute-start = (bf16[3,2,128,256]{3,2,1,0:T(8,128)(2,1)S(1)}, bf16[3,2,128,256]{3,2,1,0:T(8,128)(2,1)S(1)}, u32[]{:S(2)}, u32[]{:S(2)}) collective-permute-start(bf16[3,2,128,256]{3,2,1,0:T(8,128)(2,1)S(1)} %get-tuple-element.9), channel_id=1, source_target_pairs={{0,4},{4,8},{8,12},{12,16},{16,20},{20,24},{24,28},{28,32},{32,36}... | collective-permute-start | bytes 1179656 | tf_op jit(solution)/shard_map/ppermute | solution.py:44
  128.6 5.2 %collective-permute-done = bf16[3,2,128,256]{3,2,1,0:T(8,128)(2,1)S(1)} collective-permute-done((bf16[3,2,128,256]{3,2,1,0:T(8,128)(2,1)S(1)}, bf16[3,2,128,256]{3,2,1,0:T(8,128)(2,1)S(1)}, u32[]{:S(2)}, u32[]{:S(2)}) %collective-permute-start) | collective-permute-done | bytes 393248 | tf_op jit(solution)/shard_map/ppermute | solution.py:44
  133.9 1.4 collective-permute-start.1
  135.2 13.7 %collective-permute-done.1 = bf16[1,3,2,2,128,256]{5,4,3,2,1,0:T(8,128)(2,1)S(1)} collective-permute-done((bf16[1,3,2,2,128,256]{5,4,3,2,1,0:T(8,128)(2,1)S(1)}, bf16[1,3,2,2,128,256]{5,4,3,2,1,0:T(8,128)(2,1)S(1)}, u32[]{:S(2)}, u32[]{:S(2)}) %collective-permute-start.1) | collective-permute-done | bytes 786464 | tf_op jit(solution)/shard_map/ppermute | solution.py:24
  149.1 1.7 fusion.32
  150.8 2.9 collective-permute-start.2
  153.7 31.4 %collective-permute-done.2 = bf16[2,3,2,2,128,256]{5,4,3,2,1,0:T(8,128)(2,1)} collective-permute-done((bf16[2,3,2,2,128,256]{5,4,3,2,1,0:T(8,128)(2,1)}, bf16[2,3,2,2,128,256]{5,4,3,2,1,0:T(8,128)(2,1)}, u32[]{:S(2)}, u32[]{:S(2)}) %collective-permute-start.2) | collective-permute-done | bytes 1572896 | tf_op jit(solution)/shard_map/ppermute | solution.py:24
  185.1 1.7 pad_maximum_fusion
  186.8 0.9 multiply_reduce_fusion.1
  187.7 3.5 fusion.9
  191.2 6.9 %copy.44 = f32[4,3,2,2,128,256]{5,0,4,3,2,1:T(4,128)S(1)} copy(f32[4,3,2,2,128,256]{5,4,3,2,1,0:T(8,128)} %bitcast.79) | data formatting | bytes 12582912 | tf_op jit(solution)/shard_map/convert_element_type | solution.py:90
  198.1 4.2 %copy.49 = f32[192,8,4,256]{3,1,2,0:T(8,128)} copy(f32[192,8,4,256]{3,2,1,0:T(4,128)S(1)} %bitcast.80) | data formatting | bytes 12582912
  202.3 11.6 %convolution_convert_fusion.2 = bf16[1536,1024]{1,0:T(8,128)(2,1)} fusion(bf16[1024,1024]{1,0:T(8,128)(2,1)} %param.17, bf16[1024,1024]{1,0:T(8,128)(2,1)} %param.16, f32[1536,1024]{1,0:T(8,128)} %bitcast.76, f32[1024]{0:T(1024)S(1)} %copy-done.8, f32[1536]{0:T(1024)S(1)} %rsqrt.20), kind=kOutput, calls=%fused_computation.21 | convolution fusion | flops 6462898176 | bytes 13641728 | tf_op jit(solution)/shard_map/dot_general | solution.py:96
  213.9 1.1 copy-done.4
  215.2 88.7 %all-reduce.2.cloned.1.call-done = bf16[1536,1024]{1,0:T(8,128)(2,1)} async-done(((bf16[1536,1024]{1,0:T(8,128)(2,1)}), bf16[1536,1024]{1,0:T(8,128)(2,1)}) %all-reduce.2.cloned.1.call-update) | async-done | bytes 3145744 | tf_op jit(solution)/shard_map/psum | solution.py:95
  303.9 4.7 %multiply_reduce_fusion = f32[1536]{0:T(1024)S(1)} fusion(f32[1536,1024]{1,0:T(8,128)} %bitcast.77, bf16[1536,1024]{1,0:T(8,128)(2,1)} %all-reduce.2.cloned.1.call-done), kind=kLoop, calls=%fused_computation.13 | loop fusion | flops 6289920 | bytes 9443328 | tf_op jit(solution)/shard_map/reduce_sum | solution.py:50
  308.7 4.1 %multiply_convert_fusion = bf16[1536,1024]{1,0:T(8,128)(2,1)S(1)} fusion(f32[1536,1024]{1,0:T(8,128)} %bitcast.78, bf16[1536,1024]{1,0:T(8,128)(2,1)S(1)} %copy-done.2, f32[1024]{0:T(1024)S(1)} %copy-done.5, f32[1536]{0:T(1024)S(1)} %add_rsqrt_fusion), kind=kLoop, calls=%fused_computation.12 | loop fusion | flops 7864320 | bytes 12593152 | tf_op jit(solution)/shard_map/convert_element_type | solution.py:98
  312.8 3.6 %fusion.23 = bf16[192,8,8,128]{3,1,2,0:T(8,128)(2,1)S(1)} fusion(bf16[1536,1024]{1,0:T(8,128)(2,1)S(1)} %multiply_convert_fusion, bf16[1024,1024]{1,0:T(8,128)(2,1)S(1)} %copy-done.6), kind=kOutput, calls=%fused_computation.39 | convolution fusion | flops 3222798336 | bytes 8388608 | tf_op jit(solution)/shard_map/dot_general | solution.py:99
  316.4 3.9 %fusion.22 = bf16[192,8,8,128]{3,1,2,0:T(8,128)(2,1)S(1)} fusion(bf16[1536,1024]{1,0:T(8,128)(2,1)S(1)} %multiply_convert_fusion, bf16[1024,1024]{1,0:T(8,128)(2,1)S(1)} %copy-done.7), kind=kOutput, calls=%fused_computation.38 | convolution fusion | flops 3222798336 | bytes 8388608 | tf_op jit(solution)/shard_map/dot_general | solution.py:100
  320.3 2.5 copy.53
  323.6 1.2 fusion.15
  324.8 1.7 copy-done.3
  326.5 1.1 fusion.51
  327.7 10.4 %fusion.28 = bf16[3,2,64,8,128]{4,2,3,1,0:T(8,128)(2,1)} fusion(bf16[3,2,256,8,128]{4,3,2,1,0:T(8,128)(2,1)} %bitcast.84, f32[3,2,8,64]{3,2,1,0:T(8,128)S(1)} %fusion.51, pred[2]{0:T(512)(128)(4,1)S(1)} %add_compare_fusion, f32[3,2,8,256,64]{3,4,2,1,0:T(8,128)} %copy-done.3), kind=kOutput, calls=%fused_computation.44 | convolution fusion | flops 206048512 | bytes 7090178 | tf_op jit(solution)/shard_map/schqk,sckhd->scqhd/dot_general | solution.py:114
  338.1 1.7 copy.48
  339.8 1.2 reshape.166
  (44 shorter events, 3.0 us)
Async XLA Ops:
  6.5 2.0 copy-start
  15.9 105.0 %all-to-all-start = ((bf16[32,2,128,256]{3,2,1,0:T(8,128)(2,1)}), bf16[32,2,128,256]{3,2,1,0:T(8,128)(2,1)}, u32[]{:S(2)}, u32[]{:S(2)}) async-start(bf16[32,2,128,256]{3,2,1,0:T(8,128)(2,1)} %broadcast_select_fusion), calls=%async_computation | async-start | bytes 8388608 | tf_op jit(solution)/shard_map/all_to_all | solution.py:76
  27.9 276.0 %all-reduce.2.cloned.1.call-start = ((), (), s32[]{:S(2)}) async-start(), calls=%async_computation.1 | async-start | bytes 6291456 | tf_op jit(solution)/shard_map/psum | solution.py:95
  124.0 9.8 %collective-permute-start = (bf16[3,2,128,256]{3,2,1,0:T(8,128)(2,1)S(1)}, bf16[3,2,128,256]{3,2,1,0:T(8,128)(2,1)S(1)}, u32[]{:S(2)}, u32[]{:S(2)}) collective-permute-start(bf16[3,2,128,256]{3,2,1,0:T(8,128)(2,1)S(1)} %get-tuple-element.9), channel_id=1, source_target_pairs={{0,4},{4,8},{8,12},{12,16},{16,20},{20,24},{24,28},{28,32},{32,36}... | collective-permute-start | bytes 1179656 | tf_op jit(solution)/shard_map/ppermute | solution.py:44
  133.9 15.1 %collective-permute-start.1 = (bf16[1,3,2,2,128,256]{5,4,3,2,1,0:T(8,128)(2,1)S(1)}, bf16[1,3,2,2,128,256]{5,4,3,2,1,0:T(8,128)(2,1)S(1)}, u32[]{:S(2)}, u32[]{:S(2)}) collective-permute-start(bf16[1,3,2,2,128,256]{5,4,3,2,1,0:T(8,128)(2,1)S(1)} %get-tuple-element.8), channel_id=1, source_target_pairs={{0,1},{1,0},{2,3},{3,2},{4,5},{5,4},{6,7},{7,6},{8,9},{9,8},{10,11... | collective-permute-start | bytes 2359304 | tf_op jit(solution)/shard_map/ppermute | solution.py:24
  150.8 34.3 %collective-permute-start.2 = (bf16[2,3,2,2,128,256]{5,4,3,2,1,0:T(8,128)(2,1)}, bf16[2,3,2,2,128,256]{5,4,3,2,1,0:T(8,128)(2,1)}, u32[]{:S(2)}, u32[]{:S(2)}) collective-permute-start(bf16[2,3,2,2,128,256]{5,4,3,2,1,0:T(8,128)(2,1)} %get-tuple-element.6), channel_id=1, source_target_pairs={{0,2},{1,3},{2,0},{3,1},{4,6},{5,7},{6,4},{7,5},{8,10},{9,11},{10,... | collective-permute-start | bytes 4718600 | tf_op jit(solution)/shard_map/ppermute | solution.py:24
  198.1 4.2 %copy-start.8 = (f32[1024]{0:T(1024)S(1)}, f32[1024]{0:T(1024)}, u32[]{:S(2)}) copy-start(f32[1024]{0:T(1024)} %param.14) | copy-start | bytes 12292
  213.8 1.1 copy-start.4
  215.2 93.5 %copy-start.5 = (f32[1024]{0:T(1024)S(1)}, f32[1024]{0:T(1024)}, u32[]{:S(2)}) copy-start(f32[1024]{0:T(1024)} %param.15) | copy-start | bytes 12292
  303.9 4.8 %copy-start.2 = (bf16[1536,1024]{1,0:T(8,128)(2,1)S(1)}, bf16[1536,1024]{1,0:T(8,128)(2,1)}, u32[]{:S(2)}) copy-start(bf16[1536,1024]{1,0:T(8,128)(2,1)} %all-reduce.2.cloned.1.call-done) | copy-start | bytes 9437188
  308.7 4.1 %copy-start.6 = (bf16[1024,1024]{1,0:T(8,128)(2,1)S(1)}, bf16[1024,1024]{1,0:T(8,128)(2,1)}, u32[]{:S(2)}) copy-start(bf16[1024,1024]{1,0:T(8,128)(2,1)} %param.18) | copy-start | bytes 6291460
  312.8 3.6 %copy-start.7 = (bf16[1024,1024]{1,0:T(8,128)(2,1)S(1)}, bf16[1024,1024]{1,0:T(8,128)(2,1)}, u32[]{:S(2)}) copy-start(bf16[1024,1024]{1,0:T(8,128)(2,1)} %param.19) | copy-start | bytes 6291460
  324.8 1.7 copy-start.3
  327.7 13.3 %copy-start.1 = (bf16[32,128,256]{2,1,0:T(8,128)(2,1)S(1)}, bf16[32,128,256]{2,1,0:T(8,128)(2,1)}, u32[]{:S(2)}) copy-start(bf16[32,128,256]{2,1,0:T(8,128)(2,1)} %param.11) | copy-start | bytes 6291460
Sparse Core Ops, SparseCore 0:
  214.0 89.8 all-reduce.1
